TPU v7x, 32 devices: a whole 2x2x4 slice. The times are simulated.
32 devices in a mesh: gx: 8 (over z, x), gy: 4 (over y, core).
Axes of the slice: x: 2, y: 2, z: 4, core: 2. Of those that a mesh axis runs over, the one named last changes fastest.
Arguments:
- displacement_old: float32 [3, 64, 64, 256], P(None, 'gx', 'gy'), may hold values from -6 to 6
- pressure_old: float32 [64, 64, 256], P('gx', 'gy'), may hold values from -6 to 6
- body_force: float32 [3, 64, 64, 256], P(None, 'gx', 'gy'), may hold values from -400 to 400
- fluid_source: float32 [64, 64, 256], P('gx', 'gy'), may hold values from -400 to 400
- material_ids: int32 [64, 64, 256], P('gx', 'gy'), may hold values from 0 to 7
- materials: float32 [5, 8], replicated, may hold values from 0.5 to 4
Outputs:
- displacement: float32 [3, 64, 64, 256], P(None, 'gx', 'gy')
- pressure: float32 [64, 64, 256], P('gx', 'gy')
All inputs are finite; a program needn't handle non-finite values.
Results may differ from a plain program's by a relative error of at most 0.00017.
Values sent between devices are 32-bit elements; how exact they have to be, the bound alone decides.
A program may use at most 64 MiB of HBM per device.

v0:
```python
import jax
import jax.numpy as jnp
from jax import lax
from jax.sharding import PartitionSpec as P

OUTER = 2
INNER = 3


step_time = 4.0


def extended(shard, sides, width):
    for axis, dim in sides:
        size, length = (lax.axis_size(axis), shard.shape[dim])
        up = [(i, (i + 1) % size) for i in range(size - 1)]
        down = [(j, i) for i, j in up]
        last = lax.slice_in_dim(shard, length - width, length, axis=dim)
        first = lax.slice_in_dim(shard, 0, width, axis=dim)
        before = lax.ppermute(last, axis, up)
        after = lax.ppermute(first, axis, down)
        shard = jnp.concatenate([before, shard, after], axis=dim)
    return shard


def from_behind(shard, axis, by):
    length = lax.axis_size(axis)
    pairs = [(i, i + by) for i in range(length) if 0 <= i + by < length]
    return lax.ppermute(shard, axis, pairs)


def above_depth(values):
    return jnp.concatenate([values[..., 1:], jnp.zeros_like(values[..., :1])], axis=-1)


def below_depth(values):
    return jnp.concatenate([jnp.zeros_like(values[..., :1]), values[..., :-1]], axis=-1)


def harmonic(first_value, second_value):
    return 2.0 * first_value * second_value / (first_value + second_value)


def lookup(code_plus, materials, table_rows):
    collected = [jnp.zeros(code_plus.shape, jnp.float32) for table_row in table_rows]
    for material in range(materials.shape[1]):
        matched = code_plus == material + 1
        collected = [
            jnp.where(matched, materials[table_row, material], current)
            for table_row, current in zip(table_rows, collected)
        ]
    return collected


def run_solver(operate, precond, rhs_vec, initial):
    solution = initial
    residual = rhs_vec - operate(initial)
    direction = initial
    image_dir = initial
    gamma_last = None
    length_last = None
    for inner_step in range(INNER):
        smoothed = precond(residual)
        image_vec = operate(smoothed)
        gamma_now, delta_now = lax.psum(
            (jnp.sum(residual * smoothed), jnp.sum(smoothed * image_vec)), ("gx", "gy")
        )
        if inner_step == 0:
            step_length = gamma_now / delta_now
            direction = smoothed
            image_dir = image_vec
        else:
            ratio_now = gamma_now / gamma_last
            step_length = gamma_now / (delta_now - ratio_now * gamma_now / length_last)
            direction = smoothed + ratio_now * direction
            image_dir = image_vec + ratio_now * image_dir
        solution = solution + step_length * direction
        if inner_step + 1 < INNER:
            residual = residual - step_length * image_dir
        gamma_last = gamma_now
        length_last = step_length
    return solution


def on_device(displacement_old, pressure_old, body_force, fluid_source, material_ids, materials):
    code_plus = material_ids + 1
    widened_codes = extended(code_plus, (("gx", 0), ("gy", 1)), 1)
    lame_wide, shear_wide, perm_wide = lookup(widened_codes, materials, (0, 1, 2))
    storage, biot_raw = lookup(code_plus, materials, (3, 4))
    biot_coef = 0.25 * biot_raw
    lame_first = lame_wide[1:-1, 1:-1]
    shear_mod = shear_wide[1:-1, 1:-1]
    permeability = perm_wide[1:-1, 1:-1]
    stiff_up = [
        0.5 * (shear_mod + shear_wide[2:, 1:-1]),
        0.5 * (shear_mod + shear_wide[1:-1, 2:]),
        0.5 * (shear_mod + above_depth(shear_mod)),
    ]
    stiff_down = [
        0.5 * (shear_mod + shear_wide[:-2, 1:-1]),
        0.5 * (shear_mod + shear_wide[1:-1, :-2]),
        0.5 * (shear_mod + below_depth(shear_mod)),
    ]
    flow_up = [
        harmonic(permeability, perm_wide[2:, 1:-1]),
        harmonic(permeability, perm_wide[1:-1, 2:]),
        harmonic(permeability, above_depth(permeability)),
    ]
    flow_down = [
        harmonic(permeability, perm_wide[:-2, 1:-1]),
        harmonic(permeability, perm_wide[1:-1, :-2]),
        harmonic(permeability, below_depth(permeability)),
    ]
    stab = biot_coef * biot_coef / (lame_first + 2.0 / 3.0 * shear_mod)
    storage_total = storage + stab
    flow_sum = flow_up[0] + flow_down[0] + flow_up[1] + flow_down[1] + flow_up[2] + flow_down[2]
    inv_pressure = 1.0 / (storage_total + step_time * flow_sum)
    stiff_sum = (
        stiff_up[0] + stiff_down[0] + stiff_up[1] + stiff_down[1] + stiff_up[2] + stiff_down[2]
    )
    lame_below = [lame_wide[:-2, 1:-1], lame_wide[1:-1, :-2], below_depth(lame_first)]
    inv_blocks = 1.0 / jnp.stack([stiff_sum + lame_below[spatial] for spatial in range(3)])
    factor = lame_first / (1.0 + lame_first * (inv_blocks[0] + inv_blocks[1] + inv_blocks[2]))

    def apply_pressure(field):
        widened = extended(field, (("gx", 0), ("gy", 1)), 1)
        centre = widened[1:-1, 1:-1]
        upward = [widened[2:, 1:-1], widened[1:-1, 2:], above_depth(centre)]
        downward = [widened[:-2, 1:-1], widened[1:-1, :-2], below_depth(centre)]
        flux = jnp.zeros_like(centre)
        for spatial in range(3):
            flux = (
                flux
                + flow_up[spatial] * (centre - upward[spatial])
                + flow_down[spatial] * (centre - downward[spatial])
            )
        return storage_total * centre + step_time * flux

    def shear_part(widened):
        centre = widened[:, 1:-1, 1:-1]
        upward = [widened[:, 2:, 1:-1], widened[:, 1:-1, 2:], above_depth(centre)]
        downward = [widened[:, :-2, 1:-1], widened[:, 1:-1, :-2], below_depth(centre)]
        summed = jnp.zeros_like(centre)
        for spatial in range(3):
            summed = (
                summed
                + stiff_up[spatial] * (centre - upward[spatial])
                + stiff_down[spatial] * (centre - downward[spatial])
            )
        return (centre, summed)

    def apply_mech(field):
        widened = extended(field, (("gx", 1), ("gy", 2)), 1)
        centre, summed = shear_part(widened)
        spread = (
            widened[0, 2:, 1:-1]
            - centre[0]
            + widened[1, 1:-1, 2:]
            - centre[1]
            + above_depth(centre[2])
            - centre[2]
        )
        weighted = lame_first * spread
        below_x = jnp.concatenate([from_behind(weighted[-1:], "gx", 1), weighted[:-1]], axis=0)
        below_y = jnp.concatenate(
            [from_behind(weighted[:, -1:], "gy", 1), weighted[:, :-1]], axis=1
        )
        lame_pull = jnp.stack(
            [below_x - weighted, below_y - weighted, below_depth(weighted) - weighted]
        )
        return summed + lame_pull

    def solve_pressure(residual):
        return residual * inv_pressure

    def solve_blocks(residual):
        scaled = residual * inv_blocks
        summed = scaled[0] + scaled[1] + scaled[2]
        return scaled - inv_blocks * (factor * summed)

    pressure = pressure_old
    displacement = displacement_old
    for repeat in range(OUTER):
        change = displacement - displacement_old
        after_x = from_behind(change[0, :1], "gx", -1)
        after_y = from_behind(change[1, :, :1], "gy", -1)
        spread = (
            jnp.concatenate([change[0, 1:], after_x], axis=0)
            - change[0]
            + jnp.concatenate([change[1][:, 1:], after_y], axis=1)
            - change[1]
            + above_depth(change[2])
            - change[2]
        )
        rhs_pressure = (
            storage * pressure_old + step_time * fluid_source - biot_coef * spread + stab * pressure
        )
        pressure = run_solver(apply_pressure, solve_pressure, rhs_pressure, pressure)
        loaded = biot_coef * pressure
        before_x = from_behind(loaded[-1:], "gx", 1)
        before_y = from_behind(loaded[:, -1:], "gy", 1)
        pressure_push = jnp.stack(
            [
                jnp.concatenate([before_x, loaded[:-1]], axis=0) - loaded,
                jnp.concatenate([before_y, loaded[:, :-1]], axis=1) - loaded,
                below_depth(loaded) - loaded,
            ]
        )
        rhs_mech = body_force + pressure_push
        displacement = run_solver(apply_mech, solve_blocks, rhs_mech, displacement)
    return (displacement, pressure)


def solution(mesh):
    return jax.shard_map(
        on_device,
        mesh=mesh,
        in_specs=(
            P(None, "gx", "gy", None),
            P("gx", "gy", None),
            P(None, "gx", "gy", None),
            P("gx", "gy", None),
            P("gx", "gy", None),
            P(),
        ),
        out_specs=(P(None, "gx", "gy", None), P("gx", "gy", None)),
        check_vma=False,
    )
```

profile of v0, /device:TPU:0, one launch (start us, length us, event | category | flops | bytes accessed | tf_op | source)
XLA Modules:
  0.0 925.3 jit_solution(4338613938265542069)
XLA Ops:
  1.5 4.9 collective-permute-start.25
  10.1 5.2 collective-permute-start.2
  15.3 4.8 collective-permute-start.7
  35.2 5.4 select_select_fusion
  40.5 5.2 select_select_fusion.1
  46.0 5.2 select_select_fusion.2
  57.1 5.0 collective-permute-start.27
  62.1 11.2 %fusion.361 = (f32[8,16,256]{2,1,0:T(8,128)S(1)}, f32[8,16,256]{2,1,0:T(8,128)S(1)}, f32[8,16,256]{2,1,0:T(8,128)S(1)}, f32[8,16,256]{2,1,0:T(8,128)S(1)}, f32[8...) fusion(f32[8,16,256]{2,1,0:T(8,128)S(1)} %copy-done.12, ...), kind=kLoop, calls=%fused_computation.700 | loop fusion | flops 2916352 | bytes 4539968 | tf_op jit(solution)/shard_map/mul | solution.py:174
  74.7 5.8 collective-permute-start.11
  86.8 5.4 collective-permute-start.28
  97.9 43.1 %all-reduce.68 = (f32[]{:T(128)}, f32[]{:T(128)}) all-reduce(f32[]{:T(128)} %get-tuple-element.17, f32[]{:T(128)} %get-tuple-element.16), channel_id=1, replica_groups=mesh['gx'=8,'gy'=4] {'gx','gy'}, use_global_device_ids=true, to_apply=%region_1.2 | all-reduce | flops 2 | bytes 16 | tf_op jit(solution)/shard_map/psum | solution.py:65
  159.4 41.6 %all-reduce.67 = (f32[]{:T(128)}, f32[]{:T(128)}) all-reduce(f32[]{:T(128)} %get-tuple-element.15, f32[]{:T(128)} %get-tuple-element.14), channel_id=1, replica_groups=mesh['gx'=8,'gy'=4] {'gx','gy'}, use_global_device_ids=true, to_apply=%region_5.6 | all-reduce | flops 2 | bytes 16 | tf_op jit(solution)/shard_map/psum | solution.py:65
  222.6 42.9 %all-reduce.66 = (f32[]{:T(128)}, f32[]{:T(128)}) all-reduce(f32[]{:T(128)} %get-tuple-element.72, f32[]{:T(128)} %fusion.334), channel_id=1, replica_groups=mesh['gx'=8,'gy'=4] {'gx','gy'}, use_global_device_ids=true, to_apply=%region_9.10 | all-reduce | flops 2 | bytes 16 | tf_op jit(solution)/shard_map/psum | solution.py:65
  314.1 42.0 %all-reduce.65 = (f32[]{:T(128)}, f32[]{:T(128)}) all-reduce(f32[]{:T(128)} %get-tuple-element.9, f32[]{:T(128)} %get-tuple-element.8), channel_id=1, replica_groups=mesh['gx'=8,'gy'=4] {'gx','gy'}, use_global_device_ids=true, to_apply=%region_13.14 | all-reduce | flops 2 | bytes 16 | tf_op jit(solution)/shard_map/psum | solution.py:65
  359.6 4.8 collective-permute-start.37
  370.8 4.8 collective-permute-start.40
  381.4 41.9 %all-reduce.64 = (f32[]{:T(128)}, f32[]{:T(128)}) all-reduce(f32[]{:T(128)} %get-tuple-element.7, f32[]{:T(128)} %get-tuple-element.6), channel_id=1, replica_groups=mesh['gx'=8,'gy'=4] {'gx','gy'}, use_global_device_ids=true, to_apply=%region_17.18 | all-reduce | flops 2 | bytes 16 | tf_op jit(solution)/shard_map/psum | solution.py:65
  431.0 4.8 collective-permute-start.43
  442.2 4.8 collective-permute-start.46
  451.9 41.5 %all-reduce.63 = (f32[]{:T(128)}, f32[]{:T(128)}) all-reduce(f32[]{:T(128)} %get-tuple-element.60, f32[]{:T(128)} %fusion.116), channel_id=1, replica_groups=mesh['gx'=8,'gy'=4] {'gx','gy'}, use_global_device_ids=true, to_apply=%region_21.22 | all-reduce | flops 2 | bytes 16 | tf_op jit(solution)/shard_map/psum | solution.py:65
  509.0 5.5 collective-permute-start.55
  516.4 6.1 collective-permute-start.69
  529.8 41.9 %all-reduce.62 = (f32[]{:T(128)}, f32[]{:T(128)}) all-reduce(f32[]{:T(128)} %get-tuple-element.13, f32[]{:T(128)} %get-tuple-element.12), channel_id=1, replica_groups=mesh['gx'=8,'gy'=4] {'gx','gy'}, use_global_device_ids=true, to_apply=%region_25.26 | all-reduce | flops 2 | bytes 16 | tf_op jit(solution)/shard_map/psum | solution.py:65
  585.8 6.7 collective-permute-start.71
  594.1 40.6 %all-reduce.61 = (f32[]{:T(128)}, f32[]{:T(128)}) all-reduce(f32[]{:T(128)} %get-tuple-element.11, f32[]{:T(128)} %get-tuple-element.10), channel_id=1, replica_groups=mesh['gx'=8,'gy'=4] {'gx','gy'}, use_global_device_ids=true, to_apply=%region_29.30 | all-reduce | flops 2 | bytes 16 | tf_op jit(solution)/shard_map/psum | solution.py:65
  663.4 40.0 %all-reduce.60 = (f32[]{:T(128)}, f32[]{:T(128)}) all-reduce(f32[]{:T(128)} %get-tuple-element.52, f32[]{:T(128)} %fusion.335), channel_id=1, replica_groups=mesh['gx'=8,'gy'=4] {'gx','gy'}, use_global_device_ids=true, to_apply=%region_33.34 | all-reduce | flops 2 | bytes 16 | tf_op jit(solution)/shard_map/psum | solution.py:65
  742.0 42.7 %all-reduce.59 = (f32[]{:T(128)}, f32[]{:T(128)}) all-reduce(f32[]{:T(128)} %get-tuple-element.5, f32[]{:T(128)} %get-tuple-element.4), channel_id=1, replica_groups=mesh['gx'=8,'gy'=4] {'gx','gy'}, use_global_device_ids=true, to_apply=%region_37.38 | all-reduce | flops 2 | bytes 16 | tf_op jit(solution)/shard_map/psum | solution.py:65
  788.0 4.8 collective-permute-start.81
  799.2 4.8 collective-permute-start.84
  809.1 42.0 %all-reduce.58 = (f32[]{:T(128)}, f32[]{:T(128)}) all-reduce(f32[]{:T(128)} %get-tuple-element.3, f32[]{:T(128)} %get-tuple-element.2), channel_id=1, replica_groups=mesh['gx'=8,'gy'=4] {'gx','gy'}, use_global_device_ids=true, to_apply=%region_41.42 | all-reduce | flops 2 | bytes 16 | tf_op jit(solution)/shard_map/psum | solution.py:65
  869.0 4.8 collective-permute-start.90
  878.8 41.4 %all-reduce.57 = (f32[]{:T(128)}, f32[]{:T(128)}) all-reduce(f32[]{:T(128)} %get-tuple-element.42, f32[]{:T(128)} %fusion.117), channel_id=1, replica_groups=mesh['gx'=8,'gy'=4] {'gx','gy'}, use_global_device_ids=true, to_apply=%region_45.46 | all-reduce | flops 2 | bytes 16 | tf_op jit(solution)/shard_map/psum | solution.py:65
  (478 shorter events, 271.8 us)
Async XLA Ops:
  1.5 49.9 %collective-permute-start.25 = (f32[3,1,16,256]{3,2,1,0:T(8,128)S(1)}, f32[3,1,16,256]{3,2,1,0:T(8,128)S(1)}, u32[]{:S(2)}, u32[]{:S(2)}) collective-permute-start(f32[3,1,16,256]{3,2,1,0:T(8,128)S(1)} %get-tuple-element.159), channel_id=1, source_target_pairs={{0,4},{4,8},{8,12},{12,16},{16,20},{20,24},{24,28},{1,5},{5,9},{9,... | collective-permute-start | bytes 147464 | tf_op jit(solution)/shard_map/ppermute | solution.py:20
  6.4 45.9 %collective-permute-start.24 = (f32[3,1,16,256]{3,2,1,0:T(8,128)S(1)}, f32[3,1,16,256]{3,2,1,0:T(8,128)S(1)}, u32[]{:S(2)}, u32[]{:S(2)}) collective-permute-start(f32[3,1,16,256]{3,2,1,0:T(8,128)S(1)} %get-tuple-element.158), channel_id=1, source_target_pairs={{4,0},{8,4},{12,8},{16,12},{20,16},{24,20},{28,24},{5,1},{9,5},{13... | collective-permute-start | bytes 147464 | tf_op jit(solution)/shard_map/ppermute | solution.py:21
  8.8 16.2 %collective-permute-start.3 = (s32[1,16,256]{2,1,0:T(8,128)S(1)}, s32[1,16,256]{2,1,0:T(8,128)S(1)}, u32[]{:S(2)}, u32[]{:S(2)}) collective-permute-start(s32[1,16,256]{2,1,0:T(8,128)S(1)} %get-tuple-element.256), channel_id=1, source_target_pairs={{4,0},{8,4},{12,8},{16,12},{20,16},{24,20},{28,24},{5,1},{9,5},{13... | collective-permute-start | bytes 49160 | tf_op jit(solution)/shard_map/ppermute | solution.py:21
  10.1 16.3 %collective-permute-start.2 = (s32[1,16,256]{2,1,0:T(8,128)S(1)}, s32[1,16,256]{2,1,0:T(8,128)S(1)}, u32[]{:S(2)}, u32[]{:S(2)}) collective-permute-start(s32[1,16,256]{2,1,0:T(8,128)S(1)} %get-tuple-element.255), channel_id=1, source_target_pairs={{0,4},{4,8},{8,12},{12,16},{16,20},{20,24},{24,28},{1,5},{5,9},{9,... | collective-permute-start | bytes 49160 | tf_op jit(solution)/shard_map/ppermute | solution.py:20
  15.3 12.4 %collective-permute-start.7 = (f32[1,16,256]{2,1,0:T(8,128)S(1)}, f32[1,16,256]{2,1,0:T(8,128)S(1)}, u32[]{:S(2)}, u32[]{:S(2)}) collective-permute-start(f32[1,16,256]{2,1,0:T(8,128)S(1)} %get-tuple-element.249), channel_id=1, source_target_pairs={{0,4},{4,8},{8,12},{12,16},{16,20},{20,24},{24,28},{1,5},{5,9},{9,... | collective-permute-start | bytes 49160 | tf_op jit(solution)/shard_map/ppermute | solution.py:20
  30.8 26.3 %collective-permute-start.9 = (f32[10,1,256]{2,1,0:T(1,128)S(1)}, f32[10,1,256]{2,1,0:T(1,128)S(1)}, u32[]{:S(2)}, u32[]{:S(2)}) collective-permute-start(f32[10,1,256]{2,1,0:T(1,128)S(1)} %get-tuple-element.181), channel_id=1, source_target_pairs={{0,1},{1,2},{2,3},{4,5},{5,6},{6,7},{8,9},{9,10},{10,11},{12,13},{... | collective-permute-start | bytes 30728 | tf_op jit(solution)/shard_map/ppermute | solution.py:20
  33.8 28.3 %collective-permute-start.8 = (f32[10,1,256]{2,1,0:T(1,128)S(1)}, f32[10,1,256]{2,1,0:T(1,128)S(1)}, u32[]{:S(2)}, u32[]{:S(2)}) collective-permute-start(f32[10,1,256]{2,1,0:T(1,128)S(1)} %get-tuple-element.180), channel_id=1, source_target_pairs={{1,0},{2,1},{3,2},{5,4},{6,5},{7,6},{9,8},{10,9},{11,10},{13,12},{... | collective-permute-start | bytes 30728 | tf_op jit(solution)/shard_map/ppermute | solution.py:21
  55.6 29.8 %collective-permute-start.26 = (f32[3,10,1,256]{3,2,1,0:T(1,128)S(1)}, f32[3,10,1,256]{3,2,1,0:T(1,128)S(1)}, u32[]{:S(2)}, u32[]{:S(2)}) collective-permute-start(f32[3,10,1,256]{3,2,1,0:T(1,128)S(1)} %get-tuple-element.122), channel_id=1, source_target_pairs={{1,0},{2,1},{3,2},{5,4},{6,5},{7,6},{9,8},{10,9},{11,10},{13,12},{... | collective-permute-start | bytes 92168 | tf_op jit(solution)/shard_map/ppermute | solution.py:21
  57.1 225.1 %collective-permute-start.27 = (f32[3,10,1,256]{3,2,1,0:T(1,128)}, f32[3,10,1,256]{3,2,1,0:T(1,128)}, u32[]{:S(2)}, u32[]{:S(2)}) collective-permute-start(f32[3,10,1,256]{3,2,1,0:T(1,128)} %get-tuple-element.121), channel_id=1, source_target_pairs={{0,1},{1,2},{2,3},{4,5},{5,6},{6,7},{8,9},{9,10},{10,11},{12,13},{... | collective-permute-start | bytes 92168 | tf_op jit(solution)/shard_map/ppermute | solution.py:20
  81.9 14.5 %collective-permute-start.13 = (f32[10,1,256]{2,1,0:T(1,128)S(1)}, f32[10,1,256]{2,1,0:T(1,128)S(1)}, u32[]{:S(2)}, u32[]{:S(2)}) collective-permute-start(f32[10,1,256]{2,1,0:T(1,128)S(1)} %get-tuple-element.179), channel_id=1, source_target_pairs={{0,1},{1,2},{2,3},{4,5},{5,6},{6,7},{8,9},{9,10},{10,11},{12,13},{... | collective-permute-start | bytes 30728 | tf_op jit(solution)/shard_map/ppermute | solution.py:20
  84.2 12.3 %collective-permute-start.12 = (f32[10,1,256]{2,1,0:T(1,128)S(1)}, f32[10,1,256]{2,1,0:T(1,128)S(1)}, u32[]{:S(2)}, u32[]{:S(2)}) collective-permute-start(f32[10,1,256]{2,1,0:T(1,128)S(1)} %get-tuple-element.178), channel_id=1, source_target_pairs={{1,0},{2,1},{3,2},{5,4},{6,5},{7,6},{9,8},{10,9},{11,10},{13,12},{... | collective-permute-start | bytes 30728 | tf_op jit(solution)/shard_map/ppermute | solution.py:21
  86.8 126.6 %collective-permute-start.28 = (f32[1,16,256]{2,1,0:T(8,128)}, f32[1,16,256]{2,1,0:T(8,128)}, u32[]{:S(2)}, u32[]{:S(2)}) collective-permute-start(f32[1,16,256]{2,1,0:T(8,128)} %slice.1576), channel_id=1, source_target_pairs={{0,4},{4,8},{8,12},{12,16},{16,20},{20,24},{24,28},{1,5},{5,9},{9,... | collective-permute-start | bytes 49160 | tf_op jit(solution)/shard_map/ppermute | solution.py:29
  92.2 121.1 %collective-permute-start.29 = (f32[8,1,256]{2,1,0:T(1,128)}, f32[8,1,256]{2,1,0:T(1,128)}, u32[]{:S(2)}, u32[]{:S(2)}) collective-permute-start(f32[8,1,256]{2,1,0:T(1,128)} %slice.1578), channel_id=1, source_target_pairs={{0,1},{1,2},{2,3},{4,5},{5,6},{6,7},{8,9},{9,10},{10,11},{12,13},{... | collective-permute-start | bytes 24584 | tf_op jit(solution)/shard_map/ppermute | solution.py:29
  269.5 12.5 %collective-permute-start.22 = (f32[1,16,256]{2,1,0:T(8,128)S(1)}, f32[1,16,256]{2,1,0:T(8,128)S(1)}, u32[]{:S(2)}, u32[]{:S(2)}) collective-permute-start(f32[1,16,256]{2,1,0:T(8,128)S(1)} %slice.1558), channel_id=1, source_target_pairs={{0,4},{4,8},{8,12},{12,16},{16,20},{20,24},{24,28},{1,5},{5,9},{9,... | collective-permute-start | bytes 49160 | tf_op jit(solution)/shard_map/ppermute | solution.py:29
  276.1 18.3 %collective-permute-start.50 = (f32[1,16,256]{2,1,0:T(8,128)S(1)}, f32[1,16,256]{2,1,0:T(8,128)S(1)}, u32[]{:S(2)}, u32[]{:S(2)}) collective-permute-start(f32[1,16,256]{2,1,0:T(8,128)S(1)} %get-tuple-element.210), channel_id=1, source_target_pairs={{4,0},{8,4},{12,8},{16,12},{20,16},{24,20},{28,24},{5,1},{9,5},{13... | collective-permute-start | bytes 49160 | tf_op jit(solution)/shard_map/ppermute | solution.py:21
  277.5 16.9 %collective-permute-start.51 = (f32[1,16,256]{2,1,0:T(8,128)S(1)}, f32[1,16,256]{2,1,0:T(8,128)S(1)}, u32[]{:S(2)}, u32[]{:S(2)}) collective-permute-start(f32[1,16,256]{2,1,0:T(8,128)S(1)} %get-tuple-element.209), channel_id=1, source_target_pairs={{0,4},{4,8},{8,12},{12,16},{16,20},{20,24},{24,28},{1,5},{5,9},{9,... | collective-permute-start | bytes 49160 | tf_op jit(solution)/shard_map/ppermute | solution.py:20
  295.1 207.6 %collective-permute-start.53 = (f32[10,1,256]{2,1,0:T(1,128)}, f32[10,1,256]{2,1,0:T(1,128)S(1)}, u32[]{:S(2)}, u32[]{:S(2)}) collective-permute-start(f32[10,1,256]{2,1,0:T(1,128)} %get-tuple-element.173), channel_id=1, source_target_pairs={{0,1},{1,2},{2,3},{4,5},{5,6},{6,7},{8,9},{9,10},{10,11},{12,13},{... | collective-permute-start | bytes 30728 | tf_op jit(solution)/shard_map/ppermute | solution.py:20
  298.8 203.9 %collective-permute-start.52 = (f32[10,1,256]{2,1,0:T(1,128)}, f32[10,1,256]{2,1,0:T(1,128)S(1)}, u32[]{:S(2)}, u32[]{:S(2)}) collective-permute-start(f32[10,1,256]{2,1,0:T(1,128)} %get-tuple-element.172), channel_id=1, source_target_pairs={{1,0},{2,1},{3,2},{5,4},{6,5},{7,6},{9,8},{10,9},{11,10},{13,12},{... | collective-permute-start | bytes 30728 | tf_op jit(solution)/shard_map/ppermute | solution.py:21
  300.1 12.9 %collective-permute-start.33 = (f32[3,10,1,256]{3,2,1,0:T(1,128)S(1)}, f32[3,10,1,256]{3,2,1,0:T(1,128)S(1)}, u32[]{:S(2)}, u32[]{:S(2)}) collective-permute-start(f32[3,10,1,256]{3,2,1,0:T(1,128)S(1)} %get-tuple-element.119), channel_id=1, source_target_pairs={{0,1},{1,2},{2,3},{4,5},{5,6},{6,7},{8,9},{9,10},{10,11},{12,13},{... | collective-permute-start | bytes 92168 | tf_op jit(solution)/shard_map/ppermute | solution.py:20
  367.6 11.9 %collective-permute-start.39 = (f32[3,10,1,256]{3,2,1,0:T(1,128)S(1)}, f32[3,10,1,256]{3,2,1,0:T(1,128)S(1)}, u32[]{:S(2)}, u32[]{:S(2)}) collective-permute-start(f32[3,10,1,256]{3,2,1,0:T(1,128)S(1)} %get-tuple-element.117), channel_id=1, source_target_pairs={{0,1},{1,2},{2,3},{4,5},{5,6},{6,7},{8,9},{9,10},{10,11},{12,13},{... | collective-permute-start | bytes 92168 | tf_op jit(solution)/shard_map/ppermute | solution.py:20
  507.7 15.5 %collective-permute-start.54 = (f32[1,16,256]{2,1,0:T(8,128)S(1)}, f32[1,16,256]{2,1,0:T(8,128)S(1)}, u32[]{:S(2)}, u32[]{:S(2)}) collective-permute-start(f32[1,16,256]{2,1,0:T(8,128)S(1)} %get-tuple-element.206), channel_id=1, source_target_pairs={{4,0},{8,4},{12,8},{16,12},{20,16},{24,20},{28,24},{5,1},{9,5},{13... | collective-permute-start | bytes 49160 | tf_op jit(solution)/shard_map/ppermute | solution.py:21
  509.0 14.2 %collective-permute-start.55 = (f32[1,16,256]{2,1,0:T(8,128)S(1)}, f32[1,16,256]{2,1,0:T(8,128)S(1)}, u32[]{:S(2)}, u32[]{:S(2)}) collective-permute-start(f32[1,16,256]{2,1,0:T(8,128)S(1)} %get-tuple-element.205), channel_id=1, source_target_pairs={{0,4},{4,8},{8,12},{12,16},{16,20},{20,24},{24,28},{1,5},{5,9},{9,... | collective-permute-start | bytes 49160 | tf_op jit(solution)/shard_map/ppermute | solution.py:20
  515.1 68.0 %collective-permute-start.68 = (f32[3,1,16,256]{3,2,1,0:T(8,128)}, f32[3,1,16,256]{3,2,1,0:T(8,128)}, u32[]{:S(2)}, u32[]{:S(2)}) collective-permute-start(f32[3,1,16,256]{3,2,1,0:T(8,128)} %get-tuple-element.140), channel_id=1, source_target_pairs={{4,0},{8,4},{12,8},{16,12},{20,16},{24,20},{28,24},{5,1},{9,5},{13... | collective-permute-start | bytes 147464 | tf_op jit(solution)/shard_map/ppermute | solution.py:21
  516.4 66.7 %collective-permute-start.69 = (f32[3,1,16,256]{3,2,1,0:T(8,128)}, f32[3,1,16,256]{3,2,1,0:T(8,128)}, u32[]{:S(2)}, u32[]{:S(2)}) collective-permute-start(f32[3,1,16,256]{3,2,1,0:T(8,128)} %get-tuple-element.139), channel_id=1, source_target_pairs={{0,4},{4,8},{8,12},{12,16},{16,20},{20,24},{24,28},{1,5},{5,9},{9,... | collective-permute-start | bytes 147464 | tf_op jit(solution)/shard_map/ppermute | solution.py:20
  580.5 12.1 %collective-permute-start.61 = (f32[10,1,256]{2,1,0:T(1,128)S(1)}, f32[10,1,256]{2,1,0:T(1,128)S(1)}, u32[]{:S(2)}, u32[]{:S(2)}) collective-permute-start(f32[10,1,256]{2,1,0:T(1,128)S(1)} %get-tuple-element.169), channel_id=1, source_target_pairs={{0,1},{1,2},{2,3},{4,5},{5,6},{6,7},{8,9},{9,10},{10,11},{12,13},{... | collective-permute-start | bytes 30728 | tf_op jit(solution)/shard_map/ppermute | solution.py:20
  584.6 62.3 %collective-permute-start.70 = (f32[3,10,1,256]{3,2,1,0:T(1,128)}, f32[3,10,1,256]{3,2,1,0:T(1,128)S(1)}, u32[]{:S(2)}, u32[]{:S(2)}) collective-permute-start(f32[3,10,1,256]{3,2,1,0:T(1,128)} %get-tuple-element.114), channel_id=1, source_target_pairs={{1,0},{2,1},{3,2},{5,4},{6,5},{7,6},{9,8},{10,9},{11,10},{13,12},{... | collective-permute-start | bytes 92168 | tf_op jit(solution)/shard_map/ppermute | solution.py:21
  585.8 129.0 %collective-permute-start.71 = (f32[3,10,1,256]{3,2,1,0:T(1,128)}, f32[3,10,1,256]{3,2,1,0:T(1,128)}, u32[]{:S(2)}, u32[]{:S(2)}) collective-permute-start(f32[3,10,1,256]{3,2,1,0:T(1,128)} %get-tuple-element.113), channel_id=1, source_target_pairs={{0,1},{1,2},{2,3},{4,5},{5,6},{6,7},{8,9},{9,10},{10,11},{12,13},{... | collective-permute-start | bytes 92168 | tf_op jit(solution)/shard_map/ppermute | solution.py:20
  648.3 65.5 %collective-permute-start.73 = (f32[8,1,256]{2,1,0:T(1,128)}, f32[8,1,256]{2,1,0:T(1,128)}, u32[]{:S(2)}, u32[]{:S(2)}) collective-permute-start(f32[8,1,256]{2,1,0:T(1,128)} %slice.1686), channel_id=1, source_target_pairs={{0,1},{1,2},{2,3},{4,5},{5,6},{6,7},{8,9},{9,10},{10,11},{12,13},{... | collective-permute-start | bytes 24584 | tf_op jit(solution)/shard_map/ppermute | solution.py:29
  650.2 12.4 %collective-permute-start.65 = (f32[10,1,256]{2,1,0:T(1,128)S(1)}, f32[10,1,256]{2,1,0:T(1,128)S(1)}, u32[]{:S(2)}, u32[]{:S(2)}) collective-permute-start(f32[10,1,256]{2,1,0:T(1,128)S(1)} %get-tuple-element.167), channel_id=1, source_target_pairs={{0,1},{1,2},{2,3},{4,5},{5,6},{6,7},{8,9},{9,10},{10,11},{12,13},{... | collective-permute-start | bytes 30728 | tf_op jit(solution)/shard_map/ppermute | solution.py:20
  658.2 55.6 %collective-permute-start.72 = (f32[1,16,256]{2,1,0:T(8,128)S(1)}, f32[1,16,256]{2,1,0:T(8,128)S(1)}, u32[]{:S(2)}, u32[]{:S(2)}) collective-permute-start(f32[1,16,256]{2,1,0:T(8,128)S(1)} %slice.1684), channel_id=1, source_target_pairs={{0,4},{4,8},{8,12},{12,16},{16,20},{20,24},{24,28},{1,5},{5,9},{9,... | collective-permute-start | bytes 49160 | tf_op jit(solution)/shard_map/ppermute | solution.py:29
  727.4 13.5 %collective-permute-start.77 = (f32[3,10,1,256]{3,2,1,0:T(1,128)S(1)}, f32[3,10,1,256]{3,2,1,0:T(1,128)S(1)}, u32[]{:S(2)}, u32[]{:S(2)}) collective-permute-start(f32[3,10,1,256]{3,2,1,0:T(1,128)S(1)} %get-tuple-element.111), channel_id=1, source_target_pairs={{0,1},{1,2},{2,3},{4,5},{5,6},{6,7},{8,9},{9,10},{10,11},{12,13},{... | collective-permute-start | bytes 92168 | tf_op jit(solution)/shard_map/ppermute | solution.py:20
  865.9 11.9 %collective-permute-start.89 = (f32[3,10,1,256]{3,2,1,0:T(1,128)S(1)}, f32[3,10,1,256]{3,2,1,0:T(1,128)S(1)}, u32[]{:S(2)}, u32[]{:S(2)}) collective-permute-start(f32[3,10,1,256]{3,2,1,0:T(1,128)S(1)} %get-tuple-element.107), channel_id=1, source_target_pairs={{0,1},{1,2},{2,3},{4,5},{5,6},{6,7},{8,9},{9,10},{10,11},{12,13},{... | collective-permute-start | bytes 92168 | tf_op jit(solution)/shard_map/ppermute | solution.py:20
  (121 other events, 1803.1 us)
where the time goes:
time: 931 us; the launch traced here: 925 us
  blocking collectives  501 us (54%)
  starting transfers between devices  262 us (28%)
  other arithmetic  67.1 us (7%)
  between operations  41.9 us (5%)
  waiting for transfers between devices  32.4 us (3%)
  local copies, waits for them, and re-layouts  20.5 us (2%)
    psum x12, blocking collectives, run_solver(): lax.psum((jnp.sum(residual * smoothed), jnp.sum(smoothed * image_vec)), (...  501 us
    ppermute x34, starting transfers between devices, extended(): before = lax.ppermute(last, axis, up)  137 us
    ppermute x24, starting transfers between devices, from_behind(): return lax.ppermute(shard, axis, pairs)  80.4 us
    ppermute x34, starting transfers between devices, extended(): after = lax.ppermute(first, axis, down)  44.3 us
  transfers between devices with their start and end apart: 92, of which 20 were waited for; matrix products, arithmetic and copies ran while one was open for 8% of the time, Pallas kernels for 0%

commit v1 on v0

v1 whole, which is shorter than its diff:
```python
import functools
import jax
import jax.numpy as jnp
from jax import lax
from jax.experimental import pallas as pl
from jax.experimental.pallas import tpu as pltpu
from jax.sharding import PartitionSpec as P

OUTER = 2
INNER = 3
step_time = 4.0
MESH = pl.DeviceIdType.MESH
F32 = jnp.float32


def kernel(dims, *refs):
    ngx, ngy, nx, ny, nz, nmat = dims
    (mat, d_old, p_old, bforce, fsource, ids, d_out, p_out,
     XI, YIS, YIH, LAM, SHR, PRM, BIO, LAMY, SHRY, PRMY, BIOY, STO, STAB,
     SX, SY, SZ, SSUM, FX, FY, FZ, DIAG, PINV, HB, KF,
     PX, PYS, PYH, MX, MYS, MYH, MCS, MCH,
     WP, WM, RP, RM, AP, AD, DC, LY, RB1, RB2,
     isend, irecv, psend, precv, msend, mrecv, rsend1, rrecv1, rsend2, rrecv2) = refs
    gx, gy = lax.axis_index("gx"), lax.axis_index("gy")
    has = {(-1, 0): gx > 0, (1, 0): gx < ngx - 1, (0, -1): gy > 0, (0, 1): gy < ngy - 1}
    has[(1, -1)] = jnp.logical_and(has[(1, 0)], has[(0, -1)])
    has[(-1, 1)] = jnp.logical_and(has[(-1, 0)], has[(0, 1)])

    rows = lax.broadcasted_iota(jnp.int32, (ny, nz), 0)
    lanes = lax.broadcasted_iota(jnp.int32, (ny, nz), 1)
    lanes8 = lax.broadcasted_iota(jnp.int32, (nx, nz), 1)
    rows8 = lax.broadcasted_iota(jnp.int32, (nx, nz), 0)
    lane1 = lax.broadcasted_iota(jnp.int32, (1, 128), 1)
    first_row, last_row = rows == 0, rows == ny - 1
    first_lane, last_lane = lanes == 0, lanes == nz - 1
    zero = jnp.zeros((ny, nz), F32)
    zero8 = jnp.zeros((nx, nz), F32)

    def upz(v):
        return pltpu.roll(v, nz - 1, 1)

    def dnz(v):
        return pltpu.roll(v, 1, 1)

    def upy(v, halo):
        return jnp.where(last_row, halo, pltpu.roll(v, ny - 1, 0))

    def dny(v, halo):
        return jnp.where(first_row, halo, pltpu.roll(v, 1, 0))

    def fold(v):
        out = None
        for i in range(0, ny, 8):
            for j in range(0, nz, 128):
                part = v[i:i + 8, j:j + 128]
                out = part if out is None else out + part
        return out

    def loop(body, init, low=0, high=nx):
        return lax.fori_loop(low, high, body, init)

    def copies_of(pairs, send, recv):
        made = []
        for n, (src, dst, off) in enumerate(pairs):
            copy = pltpu.make_async_remote_copy(
                src_ref=src, dst_ref=dst, send_sem=send.at[n], recv_sem=recv.at[n],
                device_id=(gx + off[0], gy + off[1]), device_id_type=MESH)
            made.append((copy, off))
        return made

    def start(made):
        for copy, off in made:
            @pl.when(has[off])
            def _(copy=copy):
                copy.start()

    def wait_recv(made):
        for copy, off in made:
            @pl.when(has[(-off[0], -off[1])])
            def _(copy=copy):
                copy.wait_recv()

    def wait_send(made):
        for copy, off in made:
            @pl.when(has[off])
            def _(copy=copy):
                copy.wait_send()

    def scalar_field(f):
        return copies_of(
            [(PX.at[f, 1], PX.at[f, nx + 1], (-1, 0)), (PX.at[f, nx], PX.at[f, 0], (1, 0)),
             (PYS.at[f, 0], PYH.at[f, 1], (0, -1)), (PYS.at[f, 1], PYH.at[f, 0], (0, 1))],
            psend.at[f], precv.at[f])

    def vector_field(f):
        return copies_of(
            [(MX.at[f, :, 1], MX.at[f, :, nx + 1], (-1, 0)), (MX.at[f, :, nx], MX.at[f, :, 0], (1, 0)),
             (MYS.at[f, 0], MYH.at[f, 1], (0, -1)), (MYS.at[f, 1], MYH.at[f, 0], (0, 1)),
             (MCS.at[f, 0], MCH.at[f, 0], (1, -1)), (MCS.at[f, 1], MCH.at[f, 1], (-1, 1))],
            msend.at[f], mrecv.at[f])

    def put_scalar(f, i, v):
        PX[f, i + 1] = v
        PYS[f, 0, pl.ds(i, 1), :] = v[0:1]
        PYS[f, 1, pl.ds(i, 1), :] = v[ny - 1:ny]

    def put_vector(f, i, vs):
        for a in range(3):
            MX[f, a, i + 1] = vs[a]
            MYS[f, 0, a, pl.ds(i, 1), :] = vs[a][0:1]
            MYS[f, 1, a, pl.ds(i, 1), :] = vs[a][ny - 1:ny]

    def put_corners(f):
        MCS[f, 0] = MYS[f, 0, 1, nx - 1:nx, :]
        MCS[f, 1] = MYS[f, 1, 0, 0:1, :]

    nf = 1 + OUTER * INNER
    XI[0] = jnp.zeros((ny, nz), jnp.int32)
    XI[nx + 1] = jnp.zeros((ny, nz), jnp.int32)
    for s in range(2):
        YIH[s] = jnp.zeros((nx, nz), jnp.int32)

    def clear(f, c):
        PX[f, 0] = zero
        PX[f, nx + 1] = zero
        for s in range(2):
            PYH[f, s] = zero8
            MCH[f, s] = jnp.zeros((1, nz), F32)
            for a in range(3):
                MX[f, a, s * (nx + 1)] = zero
                MYH[f, s, a] = zero8
        return c
    lax.fori_loop(0, nf, clear, 0)

    barrier = pltpu.get_barrier_semaphore()
    for d in range(1, ngx):
        pl.semaphore_signal(barrier, inc=1, device_id=(lax.rem(gx + d, ngx), gy), device_id_type=MESH)
    for d in range(1, ngy):
        pl.semaphore_signal(barrier, inc=1, device_id=(gx, lax.rem(gy + d, ngy)), device_id_type=MESH)
    for off in ((1, -1), (-1, 1)):
        @pl.when(has[off])
        def _(off=off):
            pl.semaphore_signal(barrier, inc=1, device_id=(gx + off[0], gy + off[1]), device_id_type=MESH)

    def stage(i, c):
        code = ids[i] + 1
        XI[i + 1] = code
        YIS[0, pl.ds(i, 1), :] = code[0:1]
        YIS[1, pl.ds(i, 1), :] = code[ny - 1:ny]
        put_scalar(0, i, p_old[i])
        put_vector(0, i, [d_old[a, i] for a in range(3)])
        return c
    loop(stage, 0)
    put_corners(0)

    corners = has[(1, -1)].astype(jnp.int32) + has[(-1, 1)].astype(jnp.int32)
    pl.semaphore_wait(barrier, ngx - 1 + ngy - 1 + corners)

    codes_copy = copies_of(
        [(XI.at[1], XI.at[nx + 1], (-1, 0)), (XI.at[nx], XI.at[0], (1, 0)),
         (YIS.at[0], YIH.at[1], (0, -1)), (YIS.at[1], YIH.at[0], (0, 1))], isend, irecv)
    p_copy, d_copy = scalar_field(0), vector_field(0)
    start(codes_copy)
    start(p_copy)
    start(d_copy)

    def lookup(code, table_rows):
        out = [jnp.zeros(code.shape, F32) for _ in table_rows]
        for m in range(nmat):
            hit = code == m + 1
            out = [jnp.where(hit, mat[t, m], v) for t, v in zip(table_rows, out)]
        return out

    def look_plane(i, c):
        lam, shr, prm, sto, bio = lookup(XI[i + 1], (0, 1, 2, 3, 4))
        bio = 0.25 * bio
        LAM[i + 1] = lam
        SHR[i + 1] = shr
        PRM[i + 1] = prm
        BIO[i + 1] = bio
        STO[i] = sto
        STAB[i] = bio * bio / (lam + 2.0 / 3.0 * shr)
        return c
    loop(look_plane, 0)
    wait_recv(codes_copy)

    for j in (0, nx + 1):
        lam, shr, prm, bio = lookup(XI[j], (0, 1, 2, 4))
        LAM[j] = lam
        SHR[j] = shr
        PRM[j] = prm
        BIO[j] = 0.25 * bio
    for s in range(2):
        lam, shr, prm, bio = lookup(YIH[s], (0, 1, 2, 4))
        SHRY[s] = shr
        PRMY[s] = prm
        if s == 0:
            LAMY[...] = lam
            BIOY[...] = 0.25 * bio

    def harmonic(one, two):
        return (2.0 * step_time) * one * two / (one + two)

    def harmonic_plane(j, c):
        FX[j] = harmonic(PRM[j], PRM[j + 1])
        SX[j] = 0.5 * (SHR[j] + SHR[j + 1])
        return c
    loop(harmonic_plane, 0, 0, nx + 1)

    def coefs(i, c):
        shr, prm, lam = SHR[i + 1], PRM[i + 1], LAM[i + 1]
        row = pl.ds(i, 1)
        fyu = harmonic(prm, upy(prm, PRMY[1, row, :]))
        fyd = harmonic(prm, dny(prm, PRMY[0, row, :]))
        fzu = jnp.where(last_lane, 0.0, harmonic(prm, upz(prm)))
        fzd = jnp.where(first_lane, 0.0, dnz(fzu))
        FY[1, i], FY[0, i], FZ[1, i], FZ[0, i] = fyu, fyd, fzu, fzd
        diag = STO[i] + STAB[i] + (FX[i] + FX[i + 1] + fyu + fyd + fzu + fzd)
        DIAG[i] = diag
        PINV[i] = 1.0 / diag
        half = 0.5 * shr
        syu = 0.5 * (shr + upy(shr, SHRY[1, row, :]))
        syd = 0.5 * (shr + dny(shr, SHRY[0, row, :]))
        szu = half + jnp.where(last_lane, 0.0, 0.5 * upz(shr))
        szd = half + jnp.where(first_lane, 0.0, 0.5 * dnz(shr))
        total = SX[i] + SX[i + 1] + syu + syd + szu + szd
        SY[1, i], SY[0, i] = syu, syd
        SZ[1, i] = jnp.where(last_lane, 0.0, szu)
        SZ[0, i] = jnp.where(first_lane, 0.0, szd)
        SSUM[i] = total
        h0 = 1.0 / (total + LAM[i])
        h1 = 1.0 / (total + dny(lam, LAMY[row, :]))
        h2 = 1.0 / (total + jnp.where(first_lane, 0.0, dnz(lam)))
        HB[0, i], HB[1, i], HB[2, i] = h0, h1, h2
        KF[i] = lam / (1.0 + lam * (h0 + h1 + h2))
        return c
    loop(coefs, 0)

    def apply_pressure(f, emit, init):
        def body(i, c):
            row = pl.ds(i, 1)
            v = PX[f, i + 1]
            out = (DIAG[i] * v - FX[i + 1] * PX[f, i + 2] - FX[i] * PX[f, i]
                   - FY[1, i] * upy(v, PYH[f, 1, row, :]) - FY[0, i] * dny(v, PYH[f, 0, row, :])
                   - FZ[1, i] * upz(v) - FZ[0, i] * dnz(v))
            return emit(i, v, out, c)
        return loop(body, init)

    def apply_mech(f, emit, init):
        m = [MYH[f, 0, a] for a in range(3)]
        ahead = jnp.where(rows8 == nx - 1, MCH[f, 1], pltpu.roll(m[0], nx - 1, 0))
        z8 = jnp.where(lanes8 == nz - 1, 0.0, pltpu.roll(m[2], nz - 1, 1))
        LY[...] = LAMY[...] * (ahead - m[0] + MYS[f, 0, 1] - m[1] + z8 - m[2])
        m = [MX[f, a, 0] for a in range(3)]
        lprev = LAM[0] * (MX[f, 0, 1] - m[0] + upy(m[1], MCH[f, 0]) - m[1]
                          + jnp.where(last_lane, 0.0, upz(m[2])) - m[2])

        def body(i, carry):
            lprev, c = carry
            row = pl.ds(i, 1)
            ws, outs, div = [], [], None
            for a in range(3):
                w, wx = MX[f, a, i + 1], MX[f, a, i + 2]
                wy, wz = upy(w, MYH[f, 1, a, row, :]), upz(w)
                out = (SSUM[i] * w - SX[i + 1] * wx - SX[i] * MX[f, a, i]
                       - SY[1, i] * wy - SY[0, i] * dny(w, MYH[f, 0, a, row, :])
                       - SZ[1, i] * wz - SZ[0, i] * dnz(w))
                part = (wx, wy, jnp.where(last_lane, 0.0, wz))[a] - w
                div = part if div is None else div + part
                ws.append(w)
                outs.append(out)
            weighted = LAM[i + 1] * div
            below = (lprev, dny(weighted, LY[row, :]), jnp.where(first_lane, 0.0, dnz(weighted)))
            outs = [outs[a] + (below[a] - weighted) for a in range(3)]
            return weighted, emit(i, ws, outs, c)
        return loop(body, (lprev, init))[1]

    def block_solve(i, r):
        scaled = [r[a] * HB[a, i] for a in range(3)]
        tail = KF[i] * (scaled[0] + scaled[1] + scaled[2])
        return [scaled[a] - HB[a, i] * tail for a in range(3)]

    def dot3(a, b):
        return fold(a[0] * b[0] + a[1] * b[1] + a[2] * b[2])

    def all_sum(q, sums):
        row = jnp.zeros((1, 128), F32)
        for k, s in enumerate(sums):
            row = jnp.where(lane1 == k, jnp.sum(s, keepdims=True), row)
        for buf, send, recv, me, n, other in (
                (RB1, rsend1, rrecv1, gy, ngy, lambda t: (gx, t)),
                (RB2, rsend2, rrecv2, gx, ngx, lambda t: (t, gy))):
            buf[q, me] = row
            made = []
            for d in range(1, n):
                copy = pltpu.make_async_remote_copy(
                    src_ref=buf.at[q, me], dst_ref=buf.at[q, me], send_sem=send.at[q, d],
                    recv_sem=recv.at[q, d], device_id=other(lax.rem(me + d, n)), device_id_type=MESH)
                copy.start()
                made.append(copy)
            for copy in made:
                copy.wait_recv()
            for copy in made:
                copy.wait_send()
            row = buf[q, 0]
            for d in range(1, n):
                row = row + buf[q, d]
        return [row[:, k:k + 1] for k in range(len(sums))]

    def combine(t):
        n0, m0, m1, m2, m3, m4 = t
        n1 = m0 - n0
        n2 = m1 - n1
        l1, l2 = m1 / m0, m2 / m0
        d1 = m2 - l1 * m1
        e = m3 - l1 * m2
        l3 = jnp.where(d1 > 0, e / d1, 0.0)
        d2 = m4 - l2 * m2 - l3 * e
        y1 = n1 - l1 * n0
        y2 = n2 - l2 * n0 - l3 * y1
        c2 = jnp.where(d2 > 0, y2 / d2, 0.0)
        c1 = jnp.where(d1 > 0, y1 / d1, 0.0) - l3 * c2
        c0 = n0 / m0 - l1 * c1 - l2 * c2
        return c0, c1, c2

    zacc = jnp.zeros((8, 128), F32)
    wait_recv(p_copy)
    wait_send(p_copy)
    wait_send(codes_copy)

    def keep_ap(i, v, out, c):
        AP[i] = out
        return c
    apply_pressure(0, keep_ap, 0)

    def clear_change(i, c):
        DC[i] = zero
        for a in range(3):
            d_out[a, i] = d_old[a, i]
        return c
    loop(clear_change, 0)

    sent = []
    for outer in range(OUTER):
        base = 1 + INNER * outer

        def p_start(i, acc):
            rhs = (STO[i] * p_old[i] + step_time * fsource[i] - BIO[i + 1] * DC[i]
                   + STAB[i] * PX[0, i + 1])
            r = rhs - AP[i]
            u = r * PINV[i]
            put_scalar(base, i, u)
            return acc + fold(r * u)
        n0 = loop(p_start, zacc)
        made = scalar_field(base)
        start(made)
        sent.append(made)
        if outer == 0:
            wait_recv(d_copy)
            wait_send(d_copy)

            def keep_ad(i, ws, outs, c):
                for a in range(3):
                    AD[a, i] = outs[a]
                return c
            apply_mech(0, keep_ad, 0)
        sums = [n0]
        for k in range(INNER):
            wait_recv(made)

            def p_step(i, v, w, c):
                WP[k, i] = w
                even = c[0] + fold(v * w)
                if k == INNER - 1:
                    return (even,)
                u = w * PINV[i] - v
                put_scalar(base + k + 1, i, u)
                return even, c[1] + fold(u * w)
            sums += apply_pressure(base + k, p_step, (zacc,) * (1 if k == INNER - 1 else 2))
            if k < INNER - 1:
                made = scalar_field(base + k + 1)
                start(made)
                sent.append(made)
        cs = combine(all_sum(2 * outer, sums))

        def p_update(j, c):
            v = PX[0, j]
            for k in range(INNER):
                v = v + cs[k] * PX[base + k, j]
            PX[0, j] = v
            return c
        loop(p_update, 0, 0, nx + 1)
        ph = PYH[0, 0]
        for k in range(INNER):
            ph = ph + cs[k] * PYH[base + k, 0]
        PYH[0, 0] = ph
        LY[...] = BIOY[...] * ph

        def m_start(i, carry):
            before, acc = carry
            row = pl.ds(i, 1)
            load = BIO[i + 1] * PX[0, i + 1]
            below = (before, dny(load, LY[row, :]), jnp.where(first_lane, 0.0, dnz(load)))
            r = [bforce[a, i] + (below[a] - load) - AD[a, i] for a in range(3)]
            u = block_solve(i, r)
            put_vector(base, i, u)
            return load, acc + dot3(r, u)
        n0 = loop(m_start, (BIO[0] * PX[0, 0], zacc))[1]
        put_corners(base)
        made = vector_field(base)
        start(made)
        sent.append(made)

        def p_after(i, c):
            if outer == OUTER - 1:
                p_out[i] = PX[0, i + 1]
            else:
                v = AP[i]
                for k in range(INNER):
                    v = v + cs[k] * WP[k, i]
                AP[i] = v
            return c
        loop(p_after, 0)
        sums = [n0]
        for k in range(INNER):
            wait_recv(made)

            def m_step(i, v, w, c):
                if outer < OUTER - 1:
                    for a in range(3):
                        WM[k, a, i] = w[a]
                even = c[0] + dot3(v, w)
                if k == INNER - 1:
                    return (even,)
                z = block_solve(i, w)
                u = [z[a] - v[a] for a in range(3)]
                put_vector(base + k + 1, i, u)
                return even, c[1] + dot3(u, w)
            sums += apply_mech(base + k, m_step, (zacc,) * (1 if k == INNER - 1 else 2))
            if k < INNER - 1:
                put_corners(base + k + 1)
                made = vector_field(base + k + 1)
                start(made)
                sent.append(made)
        cs = combine(all_sum(2 * outer + 1, sums))

        def mixed(get):
            v = cs[0] * get(base)
            for k in range(1, INNER):
                v = v + cs[k] * get(base + k)
            return v

        def m_update(i, c):
            row = pl.ds(i, 1)
            change = [mixed(lambda f, a=a: MX[f, a, i + 1]) for a in range(3)]
            for a in range(3):
                d_out[a, i] = d_out[a, i] + change[a]
            if outer < OUTER - 1:
                for a in range(3):
                    v = AD[a, i]
                    for k in range(INNER):
                        v = v + cs[k] * WM[k, a, i]
                    AD[a, i] = v
                cx = mixed(lambda f: MX[f, 0, i + 2])
                cy = upy(change[1], mixed(lambda f: MYH[f, 1, 1, row, :]))
                cz = jnp.where(last_lane, 0.0, upz(change[2]))
                DC[i] = DC[i] + (cx - change[0] + cy - change[1] + cz - change[2])
            return c
        loop(m_update, 0)

    for made in sent:
        wait_send(made)


def on_device(dims, d_old, p_old, bforce, fsource, ids, materials):
    ngx, ngy, nx, ny, nz, nmat = dims
    nf = 1 + OUTER * INNER
    nq = 2 * OUTER

    def vm(*shape, dtype=F32):
        return pltpu.VMEM(shape, dtype)
    plane, strip = (ny, nz), (nx, nz)
    cell = (nx, ny, nz)
    ext = (nx + 2, ny, nz)
    dma = pltpu.SemaphoreType.DMA
    scratch = [
        vm(*ext, dtype=jnp.int32), vm(2, *strip, dtype=jnp.int32), vm(2, *strip, dtype=jnp.int32),
        vm(*ext), vm(*ext), vm(*ext), vm(*ext), vm(*strip), vm(2, *strip), vm(2, *strip), vm(*strip),
        vm(*cell), vm(*cell),
        vm(nx + 1, *plane), vm(2, *cell), vm(2, *cell), vm(*cell),
        vm(nx + 1, *plane), vm(2, *cell), vm(2, *cell), vm(*cell), vm(*cell),
        vm(3, *cell), vm(*cell),
        vm(nf, *ext), vm(nf, 2, *strip), vm(nf, 2, *strip),
        vm(nf, 3, *ext), vm(nf, 2, 3, *strip), vm(nf, 2, 3, *strip), vm(nf, 2, 1, nz), vm(nf, 2, 1, nz),
        vm(INNER, *cell), vm(INNER, 3, *cell), vm(8, 128), vm(8, 128), vm(*cell), vm(3, *cell), vm(*cell),
        vm(*strip), vm(nq, ngy, 1, 128), vm(nq, ngx, 1, 128),
        dma((4,)), dma((4,)), dma((nf, 4)), dma((nf, 4)), dma((nf, 6)), dma((nf, 6)),
        dma((nq, ngy)), dma((nq, ngy)), dma((nq, ngx)), dma((nq, ngx)),
    ]
    block = pl.BlockSpec(memory_space=pltpu.VMEM)
    return pl.pallas_call(
        functools.partial(kernel, dims),
        out_shape=(jax.ShapeDtypeStruct(d_old.shape, F32), jax.ShapeDtypeStruct(p_old.shape, F32)),
        in_specs=[pl.BlockSpec(memory_space=pltpu.SMEM)] + [block] * 5,
        out_specs=(block, block),
        scratch_shapes=scratch,
        compiler_params=pltpu.CompilerParams(
            collective_id=0, has_side_effects=True, vmem_limit_bytes=48 * 1024 * 1024),
        name="poro",
    )(materials, d_old, p_old, bforce, fsource, ids)


def solution(mesh):
    ngx, ngy = mesh.shape["gx"], mesh.shape["gy"]

    def body(d_old, p_old, bforce, fsource, ids, materials):
        dims = (ngx, ngy, *p_old.shape, materials.shape[1])
        return on_device(dims, d_old, p_old, bforce, fsource, ids, materials)

    return jax.shard_map(
        body,
        mesh=mesh,
        in_specs=(P(None, "gx", "gy", None), P("gx", "gy", None), P(None, "gx", "gy", None),
                  P("gx", "gy", None), P("gx", "gy", None), P()),
        out_specs=(P(None, "gx", "gy", None), P("gx", "gy", None)),
        check_vma=False,
    )
```

time: 931 us -> 111 us (0.12)
  blocking collectives: 501 us -> 0 us
  starting transfers between devices: 262 us -> 0 us
  Pallas kernels: 0 us -> 103 us
  other arithmetic: 67.1 us -> 0 us
  between operations: 41.9 us -> 0.65 us
  waiting for transfers between devices: 32.4 us -> 0 us
  local copies, waits for them, and re-layouts: 20.5 us -> 6.78 us
    psum x12 -> x0, blocking collectives: 501 us -> none  [run_solver(): lax.psum((jnp.sum(residual * smoothed), jnp.sum(smoothed * image_vec)), (...]
    ppermute x92 -> x0, starting transfers between devices: 262 us -> none  [the longest x34 137 us: extended(): before = lax.ppermute(last, axis, up)]
    pallas_call x0 -> x1, Pallas kernels: none -> 103 us  [on_device(): pl.pallas_call(functools.partial(kernel, dims), out_shape=(jax.ShapeDtype...]
    ppermute x92 -> x0, waiting for transfers between devices: 32.4 us -> none  [the longest x34 12.3 us: extended(): before = lax.ppermute(last, axis, up)]
    mul x26 -> x0, other arithmetic: 19.3 us -> none  [the longest x4 12.6 us: solve_pressure(): return residual * inv_pressure]
    reduce_sum x16 -> x0, other arithmetic: 19.1 us -> none  [the longest x12 14.2 us: run_solver(): jnp.sum(smoothed * image_vec)]
    select_n x3 -> x0, other arithmetic: 15.8 us -> none  [lookup(): jnp.where(matched, materials[table_row, material], current)]
    slice x83 -> x0, local copies, waits for them, and re-layouts: 13.9 us -> none  [the longest x26 5.99 us: above_depth(): values[..., 1:]]
  transfers between devices with their start and end apart: 92 -> 0, of which waited for: 20 -> 0; matrix products, arithmetic and copies ran while one was open for 8% -> 0% of each run, Pallas kernels for 0% -> 0%
where the time goes in v1:
time: 111 us
  Pallas kernels  103 us (93%)
  local copies, waits for them, and re-layouts  6.78 us (6%)
    pallas_call x1, Pallas kernels, on_device(): pl.pallas_call(functools.partial(kernel, dims), out_shape=(jax.ShapeDtype...  103 us
    unnamed x14, local copies, waits for them, and re-layouts  6.78 us

profile of v1, /device:TPU:0, one launch (start us, length us, event | category | flops | bytes accessed | tf_op | source)
XLA Modules:
  0.0 110.7 jit_solution(13691931272621424028)
XLA Ops:
  0.6 0.0 copy-start
  0.6 1.0 copy-done
  1.6 0.0 copy-start.1
  1.6 1.0 copy-done.1
  2.6 0.0 copy-start.2
  2.6 0.9 copy-done.2
  3.5 0.0 copy-start.3
  3.5 0.9 copy-done.3
  4.4 0.0 copy-start.4
  4.4 0.9 copy-done.4
  5.3 0.0 copy-start.5
  5.3 0.7 copy-done.5
  6.0 103.3 %poro.1 = (f32[3,8,16,256]{3,2,1,0:T(8,128)S(1)}, f32[8,16,256]{2,1,0:T(8,128)S(1)}) custom-call(f32[5,8]{1,0:T(8,128)S(1)} %copy-done.5, f32[3,8,16,256]{3,2,1,0:T(8,128)S(1)} %copy-done, f32[8,16,256]{2,1,0:T(8,128)S(1)} %copy-done.2, f32[3,8,16,256]{3,2,1,0:T(8,128)S(1)} %copy-done.1, f32[8,16,256]{2,1,0:T(8,128)S(1)} %copy-done.3, ...), custom_call_target="tpu_custom_call" | custom-call | tf_op jit(solution)/shard_map/poro/pallas_call | solution.py:501
  109.3 0.7 copy.10
  110.1 0.7 copy.11
Async XLA Ops:
  0.6 1.0 copy-start
  1.6 1.0 copy-start.1
  2.6 0.9 copy-start.2
  3.5 0.9 copy-start.3
  4.4 0.9 copy-start.4
  5.3 0.7 copy-start.5

commit v2 on v1

--- a/solution.py
+++ b/solution.py
@@ -15,12 +15,13 @@
 
 def kernel(dims, *refs):
     ngx, ngy, nx, ny, nz, nmat = dims
-    (mat, d_old, p_old, bforce, fsource, ids, d_out, p_out,
+    (mat, d_hbm, p_hbm, bf_hbm, fs_hbm, ids_hbm, d_out, p_out,
+     p_old, bforce, fsource, ids, lsem,
      XI, YIS, YIH, LAM, SHR, PRM, BIO, LAMY, SHRY, PRMY, BIOY, STO, STAB,
      SX, SY, SZ, SSUM, FX, FY, FZ, DIAG, PINV, HB, KF,
      PX, PYS, PYH, MX, MYS, MYH, MCS, MCH,
-     WP, WM, RP, RM, AP, AD, DC, LY, RB1, RB2,
-     isend, irecv, psend, precv, msend, mrecv, rsend1, rrecv1, rsend2, rrecv2) = refs
+     WP, WM, AP, AD, DC, LY, LW, RB,
+     isend, irecv, psend, precv, msend, mrecv, rsend, rrecv) = refs
     gx, gy = lax.axis_index("gx"), lax.axis_index("gy")
     has = {(-1, 0): gx > 0, (1, 0): gx < ngx - 1, (0, -1): gy > 0, (0, 1): gy < ngy - 1}
     has[(1, -1)] = jnp.logical_and(has[(1, 0)], has[(0, -1)])
@@ -56,8 +57,13 @@
                 out = part if out is None else out + part
         return out
 
-    def loop(body, init, low=0, high=nx):
-        return lax.fori_loop(low, high, body, init)
+    def loop(body, init, low=0, high=nx, half=None):
+        order = [low, high - 1] + list(range(low + 1, high - 1))
+        for n, i in enumerate(order):
+            init = body(i, init)
+            if n == 1 and half is not None:
+                half()
+        return init
 
     def copies_of(pairs, send, recv):
         made = []
@@ -68,8 +74,10 @@
             made.append((copy, off))
         return made
 
-    def start(made):
+    def start(made, along=None):
         for copy, off in made:
+            if along is not None and (off[0] != 0) != along:
+                continue
             @pl.when(has[off])
             def _(copy=copy):
                 copy.start()
@@ -101,18 +109,24 @@
 
     def put_scalar(f, i, v):
         PX[f, i + 1] = v
-        PYS[f, 0, pl.ds(i, 1), :] = v[0:1]
-        PYS[f, 1, pl.ds(i, 1), :] = v[ny - 1:ny]
+        PYS[f, 0, slice(i, i + 1), :] = v[0:1]
+        PYS[f, 1, slice(i, i + 1), :] = v[ny - 1:ny]
 
     def put_vector(f, i, vs):
         for a in range(3):
             MX[f, a, i + 1] = vs[a]
-            MYS[f, 0, a, pl.ds(i, 1), :] = vs[a][0:1]
-            MYS[f, 1, a, pl.ds(i, 1), :] = vs[a][ny - 1:ny]
+            MYS[f, 0, a, slice(i, i + 1), :] = vs[a][0:1]
+            MYS[f, 1, a, slice(i, i + 1), :] = vs[a][ny - 1:ny]
 
     def put_corners(f):
-        MCS[f, 0] = MYS[f, 0, 1, nx - 1:nx, :]
-        MCS[f, 1] = MYS[f, 1, 0, 0:1, :]
+        MCS[f, 0] = MX[f, 1, nx, 0:1, :]
+        MCS[f, 1] = MX[f, 0, 1, ny - 1:ny, :]
+
+    local = [pltpu.make_async_copy(src, dst, lsem.at[n]) for n, (src, dst) in enumerate((
+        (ids_hbm, ids), (p_hbm, PX.at[0, pl.ds(1, nx)]), (d_hbm, MX.at[0, :, pl.ds(1, nx)]),
+        (p_hbm, p_old), (fs_hbm, fsource), (bf_hbm, bforce)))]
+    for copy in local:
+        copy.start()
 
     nf = 1 + OUTER * INNER
     XI[0] = jnp.zeros((ny, nz), jnp.int32)
@@ -133,28 +147,34 @@
     lax.fori_loop(0, nf, clear, 0)
 
     barrier = pltpu.get_barrier_semaphore()
-    for d in range(1, ngx):
-        pl.semaphore_signal(barrier, inc=1, device_id=(lax.rem(gx + d, ngx), gy), device_id_type=MESH)
-    for d in range(1, ngy):
-        pl.semaphore_signal(barrier, inc=1, device_id=(gx, lax.rem(gy + d, ngy)), device_id_type=MESH)
-    for off in ((1, -1), (-1, 1)):
-        @pl.when(has[off])
-        def _(off=off):
-            pl.semaphore_signal(barrier, inc=1, device_id=(gx + off[0], gy + off[1]), device_id_type=MESH)
+    me, ndev = gx * ngy + gy, ngx * ngy
+
+    def peer(d):
+        t = lax.rem(me + d, ndev)
+        return lax.div(t, ngy), lax.rem(t, ngy)
+    for d in range(1, ndev):
+        pl.semaphore_signal(barrier, inc=1, device_id=peer(d), device_id_type=MESH)
 
     def stage(i, c):
         code = ids[i] + 1
         XI[i + 1] = code
-        YIS[0, pl.ds(i, 1), :] = code[0:1]
-        YIS[1, pl.ds(i, 1), :] = code[ny - 1:ny]
-        put_scalar(0, i, p_old[i])
-        put_vector(0, i, [d_old[a, i] for a in range(3)])
-        return c
+        YIS[0, slice(i, i + 1), :] = code[0:1]
+        YIS[1, slice(i, i + 1), :] = code[ny - 1:ny]
+        return c
+
+    def stage_values(i, c):
+        for side, y in ((0, 0), (1, ny - 1)):
+            PYS[0, side, i:i + 1, :] = PX[0, i + 1, y:y + 1, :]
+            for a in range(3):
+                MYS[0, side, a, i:i + 1, :] = MX[0, a, i + 1, y:y + 1, :]
+        return c
+    local[0].wait()
     loop(stage, 0)
+    local[1].wait()
+    local[2].wait()
+    loop(stage_values, 0)
     put_corners(0)
-
-    corners = has[(1, -1)].astype(jnp.int32) + has[(-1, 1)].astype(jnp.int32)
-    pl.semaphore_wait(barrier, ngx - 1 + ngy - 1 + corners)
+    pl.semaphore_wait(barrier, ndev - 1)
 
     codes_copy = copies_of(
         [(XI.at[1], XI.at[nx + 1], (-1, 0)), (XI.at[nx], XI.at[0], (1, 0)),
@@ -209,7 +229,7 @@
 
     def coefs(i, c):
         shr, prm, lam = SHR[i + 1], PRM[i + 1], LAM[i + 1]
-        row = pl.ds(i, 1)
+        row = slice(i, i + 1)
         fyu = harmonic(prm, upy(prm, PRMY[1, row, :]))
         fyd = harmonic(prm, dny(prm, PRMY[0, row, :]))
         fzu = jnp.where(last_lane, 0.0, harmonic(prm, upz(prm)))
@@ -236,28 +256,32 @@
         return c
     loop(coefs, 0)
 
-    def apply_pressure(f, emit, init):
+    def apply_pressure(f, emit, init, half=None):
         def body(i, c):
-            row = pl.ds(i, 1)
+            row = slice(i, i + 1)
             v = PX[f, i + 1]
             out = (DIAG[i] * v - FX[i + 1] * PX[f, i + 2] - FX[i] * PX[f, i]
                    - FY[1, i] * upy(v, PYH[f, 1, row, :]) - FY[0, i] * dny(v, PYH[f, 0, row, :])
                    - FZ[1, i] * upz(v) - FZ[0, i] * dnz(v))
             return emit(i, v, out, c)
-        return loop(body, init)
-
-    def apply_mech(f, emit, init):
+        return loop(body, init, half=half)
+
+    def apply_mech(f, emit, init, half=None):
         m = [MYH[f, 0, a] for a in range(3)]
         ahead = jnp.where(rows8 == nx - 1, MCH[f, 1], pltpu.roll(m[0], nx - 1, 0))
         z8 = jnp.where(lanes8 == nz - 1, 0.0, pltpu.roll(m[2], nz - 1, 1))
         LY[...] = LAMY[...] * (ahead - m[0] + MYS[f, 0, 1] - m[1] + z8 - m[2])
         m = [MX[f, a, 0] for a in range(3)]
-        lprev = LAM[0] * (MX[f, 0, 1] - m[0] + upy(m[1], MCH[f, 0]) - m[1]
+        below_first = LAM[0] * (MX[f, 0, 1] - m[0] + upy(m[1], MCH[f, 0]) - m[1]
                           + jnp.where(last_lane, 0.0, upz(m[2])) - m[2])
 
-        def body(i, carry):
-            lprev, c = carry
-            row = pl.ds(i, 1)
+        def weigh(i):
+            w = [MX[f, a, i + 1] for a in range(3)]
+            return LAM[i + 1] * (MX[f, 0, i + 2] - w[0] + upy(w[1], MYH[f, 1, 1, i:i + 1, :]) - w[1]
+                                 + jnp.where(last_lane, 0.0, upz(w[2])) - w[2])
+
+        def body(i, c):
+            row = slice(i, i + 1)
             ws, outs, div = [], [], None
             for a in range(3):
                 w, wx = MX[f, a, i + 1], MX[f, a, i + 2]
@@ -270,10 +294,12 @@
                 ws.append(w)
                 outs.append(out)
             weighted = LAM[i + 1] * div
-            below = (lprev, dny(weighted, LY[row, :]), jnp.where(first_lane, 0.0, dnz(weighted)))
+            LW[i] = weighted
+            before = below_first if i == 0 else weigh(i - 1) if i == nx - 1 else LW[i - 1]
+            below = (before, dny(weighted, LY[row, :]), jnp.where(first_lane, 0.0, dnz(weighted)))
             outs = [outs[a] + (below[a] - weighted) for a in range(3)]
-            return weighted, emit(i, ws, outs, c)
-        return loop(body, (lprev, init))[1]
+            return emit(i, ws, outs, c)
+        return loop(body, init, half=half)
 
     def block_solve(i, r):
         scaled = [r[a] * HB[a, i] for a in range(3)]
@@ -283,28 +309,27 @@
     def dot3(a, b):
         return fold(a[0] * b[0] + a[1] * b[1] + a[2] * b[2])
 
+    summed = []
+
     def all_sum(q, sums):
         row = jnp.zeros((1, 128), F32)
         for k, s in enumerate(sums):
             row = jnp.where(lane1 == k, jnp.sum(s, keepdims=True), row)
-        for buf, send, recv, me, n, other in (
-                (RB1, rsend1, rrecv1, gy, ngy, lambda t: (gx, t)),
-                (RB2, rsend2, rrecv2, gx, ngx, lambda t: (t, gy))):
-            buf[q, me] = row
-            made = []
-            for d in range(1, n):
-                copy = pltpu.make_async_remote_copy(
-                    src_ref=buf.at[q, me], dst_ref=buf.at[q, me], send_sem=send.at[q, d],
-                    recv_sem=recv.at[q, d], device_id=other(lax.rem(me + d, n)), device_id_type=MESH)
-                copy.start()
-                made.append(copy)
-            for copy in made:
-                copy.wait_recv()
-            for copy in made:
-                copy.wait_send()
-            row = buf[q, 0]
-            for d in range(1, n):
-                row = row + buf[q, d]
+        RB[q, me] = row
+        made = []
+        for d in range(1, ndev):
+            copy = pltpu.make_async_remote_copy(
+                src_ref=RB.at[q, me], dst_ref=RB.at[q, me], send_sem=rsend.at[q, d],
+                recv_sem=rrecv.at[q, d], device_id=peer(d), device_id_type=MESH)
+            copy.start()
+            made.append(copy)
+        for copy in made:
+            copy.wait_recv()
+        summed.extend(made)
+        parts = [RB[q, d] for d in range(ndev)]
+        while len(parts) > 1:
+            parts = [sum(parts[d + 1:d + 2], parts[d]) for d in range(0, len(parts), 2)]
+        row = parts[0]
         return [row[:, k:k + 1] for k in range(len(sums))]
 
     def combine(t):
@@ -335,10 +360,10 @@
 
     def clear_change(i, c):
         DC[i] = zero
-        for a in range(3):
-            d_out[a, i] = d_old[a, i]
         return c
     loop(clear_change, 0)
+    local[3].wait()
+    local[4].wait()
 
     sent = []
     for outer in range(OUTER):
@@ -351,10 +376,12 @@
             u = r * PINV[i]
             put_scalar(base, i, u)
             return acc + fold(r * u)
-        n0 = loop(p_start, zacc)
         made = scalar_field(base)
-        start(made)
+        n0 = loop(p_start, zacc, half=functools.partial(start, made, True))
+        start(made, False)
         sent.append(made)
+        if outer > 0:
+            loop(m_after, 0)
         if outer == 0:
             wait_recv(d_copy)
             wait_send(d_copy)
@@ -364,6 +391,7 @@
                     AD[a, i] = outs[a]
                 return c
             apply_mech(0, keep_ad, 0)
+            local[5].wait()
         sums = [n0]
         for k in range(INNER):
             wait_recv(made)
@@ -376,10 +404,13 @@
                 u = w * PINV[i] - v
                 put_scalar(base + k + 1, i, u)
                 return even, c[1] + fold(u * w)
-            sums += apply_pressure(base + k, p_step, (zacc,) * (1 if k == INNER - 1 else 2))
+            half = None
             if k < INNER - 1:
                 made = scalar_field(base + k + 1)
-                start(made)
+                half = functools.partial(start, made, True)
+            sums += apply_pressure(base + k, p_step, (zacc,) * (1 if k == INNER - 1 else 2), half)
+            if k < INNER - 1:
+                start(made, False)
                 sent.append(made)
         cs = combine(all_sum(2 * outer, sums))
 
@@ -396,19 +427,21 @@
         PYH[0, 0] = ph
         LY[...] = BIOY[...] * ph
 
-        def m_start(i, carry):
-            before, acc = carry
-            row = pl.ds(i, 1)
+        def m_start(i, acc):
+            row = slice(i, i + 1)
             load = BIO[i + 1] * PX[0, i + 1]
-            below = (before, dny(load, LY[row, :]), jnp.where(first_lane, 0.0, dnz(load)))
+            below = (BIO[i] * PX[0, i], dny(load, LY[row, :]), jnp.where(first_lane, 0.0, dnz(load)))
             r = [bforce[a, i] + (below[a] - load) - AD[a, i] for a in range(3)]
             u = block_solve(i, r)
             put_vector(base, i, u)
-            return load, acc + dot3(r, u)
-        n0 = loop(m_start, (BIO[0] * PX[0, 0], zacc))[1]
-        put_corners(base)
+            return acc + dot3(r, u)
         made = vector_field(base)
-        start(made)
+
+        def send_planes(f, made):
+            put_corners(f)
+            start(made, True)
+        n0 = loop(m_start, zacc, half=functools.partial(send_planes, base, made))
+        start(made, False)
         sent.append(made)
 
         def p_after(i, c):
@@ -436,40 +469,48 @@
                 u = [z[a] - v[a] for a in range(3)]
                 put_vector(base + k + 1, i, u)
                 return even, c[1] + dot3(u, w)
-            sums += apply_mech(base + k, m_step, (zacc,) * (1 if k == INNER - 1 else 2))
+            half = None
             if k < INNER - 1:
-                put_corners(base + k + 1)
                 made = vector_field(base + k + 1)
-                start(made)
+                half = functools.partial(send_planes, base + k + 1, made)
+            sums += apply_mech(base + k, m_step, (zacc,) * (1 if k == INNER - 1 else 2), half)
+            if k < INNER - 1:
+                start(made, False)
                 sent.append(made)
         cs = combine(all_sum(2 * outer + 1, sums))
 
-        def mixed(get):
+        def mixed(get, cs=cs, base=base):
             v = cs[0] * get(base)
             for k in range(1, INNER):
                 v = v + cs[k] * get(base + k)
             return v
 
-        def m_update(i, c):
-            row = pl.ds(i, 1)
+        def m_change(i, c):
+            row = slice(i, i + 1)
             change = [mixed(lambda f, a=a: MX[f, a, i + 1]) for a in range(3)]
+            cx = mixed(lambda f: MX[f, 0, i + 2])
+            cy = upy(change[1], mixed(lambda f: MYH[f, 1, 1, row, :]))
+            cz = jnp.where(last_lane, 0.0, upz(change[2]))
+            DC[i] = DC[i] + (cx - change[0] + cy - change[1] + cz - change[2])
+            return c
+
+        def m_after(i, c, cs=cs, mixed=mixed, outer=outer):
             for a in range(3):
-                d_out[a, i] = d_out[a, i] + change[a]
+                before = MX[0, a, i + 1] if outer == 0 else d_out[a, i]
+                d_out[a, i] = before + mixed(lambda f, a=a: MX[f, a, i + 1])
             if outer < OUTER - 1:
                 for a in range(3):
                     v = AD[a, i]
                     for k in range(INNER):
                         v = v + cs[k] * WM[k, a, i]
                     AD[a, i] = v
-                cx = mixed(lambda f: MX[f, 0, i + 2])
-                cy = upy(change[1], mixed(lambda f: MYH[f, 1, 1, row, :]))
-                cz = jnp.where(last_lane, 0.0, upz(change[2]))
-                DC[i] = DC[i] + (cx - change[0] + cy - change[1] + cz - change[2])
             return c
-        loop(m_update, 0)
+        loop(m_change if outer < OUTER - 1 else m_after, 0)
 
     for made in sent:
         wait_send(made)
+    for copy in summed:
+        copy.wait_send()
 
 
 def on_device(dims, d_old, p_old, bforce, fsource, ids, materials):
@@ -484,6 +525,7 @@
     ext = (nx + 2, ny, nz)
     dma = pltpu.SemaphoreType.DMA
     scratch = [
+        vm(*cell), vm(3, *cell), vm(*cell), vm(*cell, dtype=jnp.int32), dma((6,)),
         vm(*ext, dtype=jnp.int32), vm(2, *strip, dtype=jnp.int32), vm(2, *strip, dtype=jnp.int32),
         vm(*ext), vm(*ext), vm(*ext), vm(*ext), vm(*strip), vm(2, *strip), vm(2, *strip), vm(*strip),
         vm(*cell), vm(*cell),
@@ -492,20 +534,20 @@
         vm(3, *cell), vm(*cell),
         vm(nf, *ext), vm(nf, 2, *strip), vm(nf, 2, *strip),
         vm(nf, 3, *ext), vm(nf, 2, 3, *strip), vm(nf, 2, 3, *strip), vm(nf, 2, 1, nz), vm(nf, 2, 1, nz),
-        vm(INNER, *cell), vm(INNER, 3, *cell), vm(8, 128), vm(8, 128), vm(*cell), vm(3, *cell), vm(*cell),
-        vm(*strip), vm(nq, ngy, 1, 128), vm(nq, ngx, 1, 128),
+        vm(INNER, *cell), vm(INNER, 3, *cell), vm(*cell), vm(3, *cell), vm(*cell),
+        vm(*strip), vm(*cell), vm(nq, ngx * ngy, 1, 128),
         dma((4,)), dma((4,)), dma((nf, 4)), dma((nf, 4)), dma((nf, 6)), dma((nf, 6)),
-        dma((nq, ngy)), dma((nq, ngy)), dma((nq, ngx)), dma((nq, ngx)),
+        dma((nq, ngx * ngy)), dma((nq, ngx * ngy)),
     ]
     block = pl.BlockSpec(memory_space=pltpu.VMEM)
     return pl.pallas_call(
         functools.partial(kernel, dims),
         out_shape=(jax.ShapeDtypeStruct(d_old.shape, F32), jax.ShapeDtypeStruct(p_old.shape, F32)),
-        in_specs=[pl.BlockSpec(memory_space=pltpu.SMEM)] + [block] * 5,
+        in_specs=[pl.BlockSpec(memory_space=pltpu.SMEM)] + [pl.BlockSpec(memory_space=pl.ANY)] * 5,
         out_specs=(block, block),
         scratch_shapes=scratch,
         compiler_params=pltpu.CompilerParams(
-            collective_id=0, has_side_effects=True, vmem_limit_bytes=48 * 1024 * 1024),
+            collective_id=0, has_side_effects=True, vmem_limit_bytes=63 * 1024 * 1024),
         name="poro",
     )(materials, d_old, p_old, bforce, fsource, ids)
 

time: 111 us -> 86.3 us (0.78)
  Pallas kernels: 103 us -> 83 us
  local copies, waits for them, and re-layouts: 6.78 us -> 2.46 us
    pallas_call x1, Pallas kernels: 103 us -> 83 us  [on_device(): pl.pallas_call(functools.partial(kernel, dims), out_shape=(jax.ShapeDtype...]
    unnamed x14 -> x4, local copies, waits for them, and re-layouts: 6.78 us -> 2.46 us
where the time goes in v2:
time: 86.3 us; the launch traced here: 86.1 us
  Pallas kernels  83 us (96%)
  local copies, waits for them, and re-layouts  2.46 us (3%)
    pallas_call x1, Pallas kernels, on_device(): pl.pallas_call(functools.partial(kernel, dims), out_shape=(jax.ShapeDtype...  83 us
    unnamed x4, local copies, waits for them, and re-layouts  2.46 us

profile of v2, /device:TPU:0, one launch (start us, length us, event | category | flops | bytes accessed | tf_op | source)
XLA Modules:
  0.0 86.1 jit_solution(15367168171536378617)
XLA Ops:
  0.6 83.0 %poro.1 = (f32[3,8,16,256]{3,2,1,0:T(8,128)}, f32[8,16,256]{2,1,0:T(8,128)}) custom-call(f32[5,8]{1,0:T(8,128)} %refs_0_.1, f32[3,8,16,256]{3,2,1,0:T(8,128)} %refs_1_.1, f32[8,16,256]{2,1,0:T(8,128)} %refs_2_.1, f32[3,8,16,256]{3,2,1,0:T(8,128)} %refs_3_.1, f32[8,16,256]{2,1,0:T(8,128)} %refs_4_.1, s32[8,16,256]{2,1,0:T(8,128)} %refs_5_.1), custom_call_target="tpu_custom_call" | custom-call | tf_op jit(solution)/shard_map/poro/pallas_call | solution.py:543
  83.7 0.0 copy-start
  83.7 1.8 %copy.10 = f32[3,8,16,256]{3,2,1,0:T(8,128)} copy(f32[3,8,16,256]{3,2,1,0:T(8,128)} %get-tuple-element.4) | data formatting | bytes 786432
  85.5 0.0 copy-done
  85.5 0.7 copy.11
Async XLA Ops:
  83.7 1.8 %copy-start = (f32[8,16,256]{2,1,0:T(8,128)S(1)}, f32[8,16,256]{2,1,0:T(8,128)}, u32[]{:S(2)}) copy-start(f32[8,16,256]{2,1,0:T(8,128)} %get-tuple-element.5) | copy-start | bytes 393220

commit v3 on v2

--- a/solution.py
+++ b/solution.py
@@ -317,7 +317,7 @@
             row = jnp.where(lane1 == k, jnp.sum(s, keepdims=True), row)
         RB[q, me] = row
         made = []
-        for d in range(1, ndev):
+        for d in sorted(range(1, ndev), key=lambda d: -min(d, ndev - d)):
             copy = pltpu.make_async_remote_copy(
                 src_ref=RB.at[q, me], dst_ref=RB.at[q, me], send_sem=rsend.at[q, d],
                 recv_sem=rrecv.at[q, d], device_id=peer(d), device_id_type=MESH)
@@ -370,6 +370,8 @@
         base = 1 + INNER * outer
 
         def p_start(i, acc):
+            if outer > 0:
+                m_change(i, 0)
             rhs = (STO[i] * p_old[i] + step_time * fsource[i] - BIO[i + 1] * DC[i]
                    + STAB[i] * PX[0, i + 1])
             r = rhs - AP[i]
@@ -394,6 +396,7 @@
             local[5].wait()
         sums = [n0]
         for k in range(INNER):
+            sums = [jnp.sum(v, keepdims=True) for v in sums]
             wait_recv(made)
 
             def p_step(i, v, w, c):
@@ -456,6 +459,7 @@
         loop(p_after, 0)
         sums = [n0]
         for k in range(INNER):
+            sums = [jnp.sum(v, keepdims=True) for v in sums]
             wait_recv(made)
 
             def m_step(i, v, w, c):
@@ -505,7 +509,8 @@
                         v = v + cs[k] * WM[k, a, i]
                     AD[a, i] = v
             return c
-        loop(m_change if outer < OUTER - 1 else m_after, 0)
+        if outer == OUTER - 1:
+            loop(m_after, 0)
 
     for made in sent:
         wait_send(made)

time: 86.3 us -> 86 us (level)
  no operation moved by 1% of the time
where the time goes in v3:
time: 86 us; the launch traced here: 85.8 us
  Pallas kernels  82.7 us (96%)
  local copies, waits for them, and re-layouts  2.46 us (3%)
    pallas_call x1, Pallas kernels, on_device(): pl.pallas_call(functools.partial(kernel, dims), out_shape=(jax.ShapeDtype...  82.7 us
    unnamed x4, local copies, waits for them, and re-layouts  2.46 us

profile of v3, /device:TPU:0, one launch (start us, length us, event | category | flops | bytes accessed | tf_op | source)
XLA Modules:
  0.0 85.8 jit_solution(4796176803451740282)
XLA Ops:
  0.6 82.7 %poro.1 = (f32[3,8,16,256]{3,2,1,0:T(8,128)}, f32[8,16,256]{2,1,0:T(8,128)}) custom-call(f32[5,8]{1,0:T(8,128)} %refs_0_.1, f32[3,8,16,256]{3,2,1,0:T(8,128)} %refs_1_.1, f32[8,16,256]{2,1,0:T(8,128)} %refs_2_.1, f32[3,8,16,256]{3,2,1,0:T(8,128)} %refs_3_.1, f32[8,16,256]{2,1,0:T(8,128)} %refs_4_.1, s32[8,16,256]{2,1,0:T(8,128)} %refs_5_.1), custom_call_target="tpu_custom_call" | custom-call | tf_op jit(solution)/shard_map/poro/pallas_call | solution.py:548
  83.3 0.0 copy-start
  83.3 1.8 %copy.10 = f32[3,8,16,256]{3,2,1,0:T(8,128)} copy(f32[3,8,16,256]{3,2,1,0:T(8,128)} %get-tuple-element.4) | data formatting | bytes 786432
  85.1 0.0 copy-done
  85.1 0.7 copy.11
Async XLA Ops:
  83.3 1.8 %copy-start = (f32[8,16,256]{2,1,0:T(8,128)S(1)}, f32[8,16,256]{2,1,0:T(8,128)}, u32[]{:S(2)}) copy-start(f32[8,16,256]{2,1,0:T(8,128)} %get-tuple-element.5) | copy-start | bytes 393220
